TPU v7x, 32 devices: a whole 2x2x4 slice. The times are simulated.
32 devices in a mesh: farcp: 2 (over x), nearcp: 4 (over y, core), model: 4 (over z).
Axes of the slice: x: 2, y: 2, z: 4, core: 2. Of those that a mesh axis runs over, the one named last changes fastest.
Arguments:
- raw_keys: bfloat16 [8, 8192, 8, 128], P(None, ('farcp', 'nearcp'), 'model'), may hold values from -6 to 6
- raw_values: bfloat16 [8, 8192, 8, 128], P(None, ('farcp', 'nearcp'), 'model'), may hold values from -6 to 6
- turn_angle: float32 [8192, 64], replicated, may hold values from -3.140625 to 3.140625
- key_gain: float32 [128], replicated, may hold values from 0.25 to 1.75
Outputs:
- stored_keys: bfloat16 [8, 8192, 8, 128], P(('farcp', 'nearcp'), None, 'model')
- stored_values: bfloat16 [8, 8192, 8, 128], P(('farcp', 'nearcp'), None, 'model')
- key_scale: float32 [8, 8, 128], P(('farcp', 'nearcp'), 'model')
All inputs are finite; a program needn't handle non-finite values. Where the computation divides by a largest or mean magnitude, that divisor is 1e-20 or more.
Results may differ from a plain program's by a relative error of at most 0.001.
Values may be sent and summed in bfloat16 or wider, within the bound.
A program may use at most 192 MiB of HBM per device.

v0:
```python
import jax
import jax.numpy as jnp
from jax import lax
from jax.sharding import PartitionSpec as P


def apply_rotary(vectors, angle):
    half = vectors.shape[-1] // 2
    cosine, sine = (jnp.cos(angle)[None, :, None, :], jnp.sin(angle)[None, :, None, :])
    first, second = (vectors[..., :half], vectors[..., half:])
    return jnp.concatenate(
        [first * cosine - second * sine, second * cosine + first * sine], axis=-1
    )


def scale_rows(vectors, row_gain):
    return (
        vectors * lax.rsqrt(jnp.mean(vectors * vectors, axis=-1, keepdims=True) + 1e-06) * row_gain
    )


def prepare_keys(plain_keys, angle, key_gain):
    wide_keys = plain_keys.astype(jnp.float32)
    wide_keys = scale_rows(wide_keys, key_gain)
    return apply_rotary(wide_keys, angle)


def local(raw_keys, raw_values, turn_angle, key_gain):
    moved_keys, stored_values = (
        lax.all_to_all(raw_keys, ("farcp", "nearcp"), split_axis=0, concat_axis=1, tiled=True),
        lax.all_to_all(raw_values, ("farcp", "nearcp"), split_axis=0, concat_axis=1, tiled=True),
    )
    turned_keys = prepare_keys(moved_keys, turn_angle, key_gain)
    key_scale = jnp.max(jnp.abs(turned_keys), axis=1)
    narrow_keys = (turned_keys / key_scale[:, None]).astype(jnp.bfloat16)
    return (narrow_keys, stored_values, key_scale)


def solution(mesh):
    in_specs = (
        P(None, ("farcp", "nearcp"), "model", None),
        P(None, ("farcp", "nearcp"), "model", None),
        P(),
        P(),
    )
    out_specs = (
        P(("farcp", "nearcp"), None, "model", None),
        P(("farcp", "nearcp"), None, "model", None),
        P(("farcp", "nearcp"), "model", None),
    )
    return jax.shard_map(local, mesh=mesh, in_specs=in_specs, out_specs=out_specs, check_vma=False)
```

profile of v0, /device:TPU:0, one launch (start us, length us, event | category | flops | bytes accessed | tf_op | source)
XLA Modules:
  0.0 147.5 jit_solution(12584620178132764666)
XLA Ops:
  0.6 5.2 %all-to-all-start = ((bf16[8,1024,2,128]{3,2,1,0:T(2,128)(2,1)}), bf16[8,1024,2,128]{3,2,1,0:T(2,128)(2,1)}, u32[]{:S(2)}, u32[]{:S(2)}) async-start(bf16[8,1024,2,128]{3,2,1,0:T(2,128)(2,1)} %param.4), calls=%async_computation | async-start | bytes 8388608 | tf_op jit(solution)/shard_map/all_to_all | solution.py:30
  5.8 9.4 %fusion.1 = (f32[8192,64]{0,1:T(8,128)}, f32[8192,64]{0,1:T(8,128)S(1)}) fusion(f32[8192,64]{0,1:T(8,128)} %param.6), kind=kLoop, calls=%fused_computation.9 | loop fusion | bytes 6291456 | tf_op jit(solution)/shard_map/cos | solution.py:9
  15.2 3.8 %copy.7 = f32[8192,64]{1,0:T(8,128)} copy(f32[8192,64]{0,1:T(8,128)} %get-tuple-element.5) | data formatting | bytes 4194304 | tf_op jit(solution)/shard_map/cos | solution.py:9
  19.0 2.8 %copy.8 = f32[8192,64]{1,0:T(8,128)} copy(f32[8192,64]{0,1:T(8,128)S(1)} %get-tuple-element.6) | data formatting | bytes 4194304 | tf_op jit(solution)/shard_map/sin | solution.py:9
  21.8 32.3 %all-to-all-done = bf16[8,1024,2,128]{3,2,1,0:T(2,128)(2,1)} async-done(((bf16[8,1024,2,128]{3,2,1,0:T(2,128)(2,1)}), bf16[8,1024,2,128]{3,2,1,0:T(2,128)(2,1)}, u32[]{:S(2)}, u32[]{:S(2)}) %all-to-all-start) | async-done | bytes 4194336 | tf_op jit(solution)/shard_map/all_to_all | solution.py:30
  54.1 4.6 %all-to-all-start.1 = ((bf16[8,1024,2,128]{3,2,1,0:T(2,128)(2,1)}), bf16[8,1024,2,128]{3,2,1,0:T(2,128)(2,1)}, u32[]{:S(2)}, u32[]{:S(2)}) async-start(bf16[8,1024,2,128]{3,2,1,0:T(2,128)(2,1)} %param.5), calls=%async_computation.1 | async-start | bytes 8388608 | tf_op jit(solution)/shard_map/all_to_all | solution.py:31
  58.7 10.6 %multiply_reduce_fusion = f32[8,1024,2]{2,1,0:T(8,128)S(1)} fusion(bf16[8,1024,2,128]{3,2,1,0:T(2,128)(2,1)} %all-to-all-done), kind=kLoop, calls=%fused_computation.6 | loop fusion | flops 6275072 | bytes 4259840 | tf_op jit(solution)/shard_map/reduce_sum | solution.py:18
  69.3 2.6 %add_rsqrt_fusion = f32[8,1024,2]{2,1,0:T(8,128)} fusion(f32[8,1024,2]{2,1,0:T(8,128)S(1)} %multiply_reduce_fusion), kind=kLoop, calls=%fused_computation.8 | loop fusion | flops 32768 | bytes 131072 | tf_op jit(solution)/shard_map/rsqrt | solution.py:18
  71.9 0.0 copy-start.4
  71.9 8.3 %convert_element_type.34 = f32[8,1024,2,128]{3,2,1,0:T(2,128)} convert(bf16[8,1024,2,128]{3,2,1,0:T(2,128)(2,1)} %all-to-all-done) | non-fusion elementwise | flops 2097152 | bytes 12582912 | tf_op jit(solution)/shard_map/convert_element_type | solution.py:23
  80.2 0.0 copy-done.4
  80.2 0.0 copy-start.2
  80.2 17.6 %fusion = f32[1,8192,2,128]{3,2,1,0:T(2,128)} fusion(f32[128]{0:T(128)S(1)} %copy-done.4, f32[8192,2]{1,0:T(8,128)} %bitcast.9, f32[1,8192,2,128]{3,2,1,0:T(2,128)} %bitcast.8), kind=kLoop, calls=%fused_computation.2 | loop fusion | flops 4194304 | bytes 16843264 | tf_op jit(solution)/shard_map/mul | solution.py:18
  97.8 0.0 copy-done.2
  97.9 19.0 %multiply_subtract_fusion = (f32[1,8192,2,64]{3,2,1,0:T(2,128)}, f32[1,8192,2,64]{3,2,1,0:T(2,128)}) fusion(f32[1,8192,2,128]{3,2,1,0:T(2,128)} %fusion, f32[8192,64]{1,0:T(8,128)} %copy.8, f32[8192,64]{1,0:T(8,128)S(1)} %copy-done.2), kind=kLoop, calls=%fused_computation.5 | loop fusion | flops 6291456 | bytes 20971520 | tf_op jit(solution)/shard_map/sub | solution.py:12
  116.9 0.0 copy-start.1
  116.9 12.7 %abs_reduce_fusion = f32[2,128]{1,0:T(2,128)S(1)} fusion(f32[1,8192,2,64]{3,2,1,0:T(2,128)} %get-tuple-element.4, f32[1,8192,2,64]{3,2,1,0:T(2,128)} %get-tuple-element.3), kind=kLoop, calls=%fused_computation.3 | loop fusion | flops 6291200 | bytes 8389632 | tf_op jit(solution)/shard_map/reduce_max | solution.py:34
  129.6 0.0 copy-done
  129.6 0.0 copy-done.1
  129.6 0.0 copy-start.3
  129.6 10.2 %divide_convert_fusion = bf16[1,8192,2,128]{3,2,1,0:T(2,128)(2,1)} fusion(f32[2,128]{1,0:T(2,128)S(1)} %abs_reduce_fusion, f32[1,8192,2,64]{3,2,1,0:T(2,128)S(1)} %copy-done.1, f32[1,8192,2,64]{3,2,1,0:T(2,128)S(1)} %copy-done), kind=kLoop, calls=%fused_computation.7 | loop fusion | flops 6291456 | bytes 12583936 | tf_op jit(solution)/shard_map/convert_element_type | solution.py:35
  139.8 0.0 copy-done.3
  139.8 0.0 all-to-all-done.1
  139.8 7.7 %copy.10 = bf16[1,8192,2,128]{3,2,1,0:T(2,128)(2,1)} copy(bf16[1,8192,2,128]{3,2,1,0:T(2,128)(2,1)} %bitcast.2) | data formatting | bytes 8388608
  (1 shorter events, 0.0 us)
Async XLA Ops:
  0.6 53.5 %all-to-all-start = ((bf16[8,1024,2,128]{3,2,1,0:T(2,128)(2,1)}), bf16[8,1024,2,128]{3,2,1,0:T(2,128)(2,1)}, u32[]{:S(2)}, u32[]{:S(2)}) async-start(bf16[8,1024,2,128]{3,2,1,0:T(2,128)(2,1)} %param.4), calls=%async_computation | async-start | bytes 8388608 | tf_op jit(solution)/shard_map/all_to_all | solution.py:30
  54.1 85.6 %all-to-all-start.1 = ((bf16[8,1024,2,128]{3,2,1,0:T(2,128)(2,1)}), bf16[8,1024,2,128]{3,2,1,0:T(2,128)(2,1)}, u32[]{:S(2)}, u32[]{:S(2)}) async-start(bf16[8,1024,2,128]{3,2,1,0:T(2,128)(2,1)} %param.5), calls=%async_computation.1 | async-start | bytes 8388608 | tf_op jit(solution)/shard_map/all_to_all | solution.py:31
  71.9 8.3 %copy-start.4 = (f32[128]{0:T(128)S(1)}, f32[128]{0:T(128)}, u32[]{:S(2)}) copy-start(f32[128]{0:T(128)} %param.7) | copy-start | bytes 1540
  80.2 17.7 %copy-start.2 = (f32[8192,64]{1,0:T(8,128)S(1)}, f32[8192,64]{1,0:T(8,128)}, u32[]{:S(2)}) copy-start(f32[8192,64]{1,0:T(8,128)} %copy.7) | copy-start | bytes 6291460
  116.9 12.7 %copy-start = (f32[1,8192,2,64]{3,2,1,0:T(2,128)S(1)}, f32[1,8192,2,64]{3,2,1,0:T(2,128)}, u32[]{:S(2)}) copy-start(f32[1,8192,2,64]{3,2,1,0:T(2,128)} %get-tuple-element.3) | copy-start | bytes 12582916
  116.9 12.7 %copy-start.1 = (f32[1,8192,2,64]{3,2,1,0:T(2,128)S(1)}, f32[1,8192,2,64]{3,2,1,0:T(2,128)}, u32[]{:S(2)}) copy-start(f32[1,8192,2,64]{3,2,1,0:T(2,128)} %get-tuple-element.4) | copy-start | bytes 12582916
  129.6 10.2 %copy-start.3 = (f32[2,128]{1,0:T(2,128)}, f32[2,128]{1,0:T(2,128)S(1)}, u32[]{:S(2)}) copy-start(f32[2,128]{1,0:T(2,128)S(1)} %abs_reduce_fusion) | copy-start | bytes 3076
where the time goes:
time: 148 us; the launch traced here: 147 us
  other arithmetic  81 us (55%)
  waiting for transfers between devices  32.3 us (22%)
  local copies, waits for them, and re-layouts  23.7 us (16%)
  starting transfers between devices  9.8 us (7%)
    all_to_all x1, waiting for transfers between devices, local(): lax.all_to_all(raw_keys, ('farcp', 'nearcp'), split_axis=0, concat_axis=1...  32.3 us
    sub x1, other arithmetic, apply_rotary(): first * cosine - second * sine  19 us
    mul x1, other arithmetic, scale_rows(): vectors * lax.rsqrt(jnp.mean(vectors * vectors, axis=-1, keepdims=True) +...  17.6 us
    cos x2, local copies, waits for them, and re-layouts, apply_rotary(): jnp.cos(angle)[None, :, None, :]  13.2 us
    reduce_max x1, other arithmetic, local(): key_scale = jnp.max(jnp.abs(turned_keys), axis=1)  12.7 us
    reduce_sum x1, other arithmetic, scale_rows(): jnp.mean(vectors * vectors, axis=-1, keepdims=True) + 1e-06  10.6 us
    convert_element_type x1, other arithmetic, local(): narrow_keys = (turned_keys / key_scale[:, None]).astype(jnp.bfloat16)  10.2 us
    convert_element_type x1, other arithmetic, prepare_keys(): wide_keys = plain_keys.astype(jnp.float32)  8.3 us
  transfers between devices with their start and end apart: 2, of which 1 were waited for; matrix products, arithmetic and copies ran while one was open for 66% of the time, Pallas kernels for 0%

commit v1 on v0

v1 whole, which is shorter than its diff:
```python
import functools

import jax
import jax.numpy as jnp
from jax import lax
from jax.experimental import pallas as pl
from jax.experimental.pallas import tpu as pltpu
from jax.sharding import PartitionSpec as P

FAR, NEAR = "farcp", "nearcp"
MESH_ID = pl.DeviceIdType.MESH
TILE = 256
LANES = 128


def moved_index(index, step, size, sign):
    if size & (size - 1):
        return (index + sign * step + size) % size
    bit = 1
    while bit < size:
        if step & bit:
            index = index + bit - 2 * bit * ((index // bit) % 2)
        bit *= 2
    return index


def partner_steps(far_size, near_size):
    steps = [(f, n) for f in range(far_size) for n in range(near_size) if (f, n) != (0, 0)]
    return sorted(steps, key=lambda s: (-((s[0] > 0) + (s[1] > 1)), s))


def exchange_kernel(
    far_size, near_size, heads, keys_ref, values_ref, angle_ref, gain_ref,
    out_keys, out_values, out_scale,
    landed, cos_table, sin_table, turned, send_sem, recv_sem, local_sem,
):
    far, near = lax.axis_index(FAR), lax.axis_index(NEAR)
    me = far * near_size + near
    rows = keys_ref.shape[1]
    total_rows = landed.shape[0]
    half = angle_ref.shape[0]
    steps = partner_steps(far_size, near_size)

    def device(step, sign):
        return (
            moved_index(far, step[0], far_size, sign),
            moved_index(near, step[1], near_size, sign),
        )

    barrier = pltpu.get_barrier_semaphore()
    for step in steps:
        f, n = device(step, 1)
        pl.semaphore_signal(barrier, inc=1, device_id={FAR: f, NEAR: n}, device_id_type=MESH_ID)
    own = [
        pltpu.make_async_copy(src.at[me], dst.at[pl.ds(me * rows, rows)], local_sem.at[i])
        for i, (src, dst) in enumerate(((keys_ref, landed), (values_ref, out_values)))
    ]
    for copy in own:
        copy.start()
    pl.semaphore_wait(barrier, len(steps))

    copies = [[], []]
    for which, (src, dst) in enumerate(((keys_ref, landed), (values_ref, out_values))):
        for i, step in enumerate(steps):
            f, n = device(step, 1)
            copy = pltpu.make_async_remote_copy(
                src_ref=src.at[f * near_size + n],
                dst_ref=dst.at[pl.ds(me * rows, rows)],
                send_sem=send_sem.at[which, i],
                recv_sem=recv_sem.at[which, i],
                device_id={FAR: f, NEAR: n},
                device_id_type=MESH_ID,
            )
            copy.start()
            copies[which].append(copy)

    gain = gain_ref[...]
    other_gain = pltpu.roll(gain, half, 1)

    def fill(block, carry):
        angle = angle_ref[:, pl.ds(pl.multiple_of(block * LANES, LANES), LANES)]
        cosine, sine = jnp.cos(angle), jnp.sin(angle)
        cosine = jnp.concatenate([cosine, cosine], axis=0).T * gain
        sine = jnp.concatenate([-sine, sine], axis=0).T * other_gain
        for head in range(heads):
            place = pl.ds(block * (LANES * heads) + head, LANES, stride=heads)
            cos_table[place, :] = cosine
            sin_table[place, :] = sine
        return carry

    lax.fori_loop(0, total_rows // (heads * LANES), fill, 0)

    def prepare(owner, largest):
        def body(i, largest):
            place = pl.ds(pl.multiple_of(owner * rows + i * TILE, TILE), TILE)
            x = landed[place, :].astype(jnp.float32)
            mean = jnp.sum(x * x, axis=-1, keepdims=True) * (1.0 / x.shape[-1])
            x = x * lax.rsqrt(mean + 1e-06)
            t = x * cos_table[place, :] + pltpu.roll(x, half, 1) * sin_table[place, :]
            turned[place, :] = t
            return jnp.maximum(largest, jnp.max(jnp.abs(t).reshape(TILE // 8, 8, LANES), axis=0))

        return lax.fori_loop(0, rows // TILE, body, largest)

    largest = jnp.zeros((8, LANES), jnp.float32)
    own[0].wait()
    largest = prepare(me, largest)
    for i in reversed(range(len(steps))):
        copies[0][i].wait_recv()
        f, n = device(steps[i], -1)
        largest = prepare(f * near_size + n, largest)

    head_of = lax.broadcasted_iota(jnp.int32, (8, LANES), 0) % heads
    scale = jnp.zeros((8, LANES), jnp.float32)
    for head in range(heads):
        top = jnp.max(jnp.where(head_of == head, largest, 0.0), axis=0, keepdims=True)
        out_scale[pl.ds(head, 1), :] = top
        scale = jnp.where(head_of == head, top, scale)
    inverse = (1.0 / scale)[None]

    def narrow(i, carry):
        place = pl.ds(pl.multiple_of(i * TILE, TILE), TILE)
        t = turned[place, :].reshape(TILE // 8, 8, LANES) * inverse
        out_keys[place, :] = t.reshape(TILE, LANES).astype(out_keys.dtype)
        return carry

    lax.fori_loop(0, total_rows // TILE, narrow, 0)

    own[1].wait()
    for copy in copies[1]:
        copy.wait_recv()
    for group in copies:
        for copy in group:
            copy.wait_send()


def place_kernel(keys_ref, values_ref, out_keys, out_values, sem):
    copies = [
        pltpu.make_async_copy(keys_ref, out_keys, sem.at[0]),
        pltpu.make_async_copy(values_ref, out_values, sem.at[1]),
    ]
    for copy in copies:
        copy.start()
    for copy in copies:
        copy.wait()


def local(far_size, near_size, raw_keys, raw_values, turn_angle, key_gain):
    sequences, positions, heads, size = raw_keys.shape
    devices = far_size * near_size
    rows = positions * heads
    total = rows * devices
    steps = devices - 1
    flat = (sequences, rows, size)
    whole = pltpu.VMEM((total, size), raw_keys.dtype)
    keys, values, scale = pl.pallas_call(
        functools.partial(exchange_kernel, far_size, near_size, heads),
        out_shape=(whole, whole, jax.ShapeDtypeStruct((heads, size), jnp.float32)),
        in_specs=[
            pl.BlockSpec(memory_space=pl.ANY),
            pl.BlockSpec(memory_space=pl.ANY),
            pl.BlockSpec(memory_space=pltpu.VMEM),
            pl.BlockSpec(memory_space=pltpu.VMEM),
        ],
        out_specs=(
            pl.BlockSpec(memory_space=pltpu.VMEM),
            pl.BlockSpec(memory_space=pltpu.VMEM),
            pl.BlockSpec(memory_space=pltpu.VMEM),
        ),
        scratch_shapes=[
            pltpu.VMEM((total, size), raw_keys.dtype),
            pltpu.VMEM((total, size), jnp.float32),
            pltpu.VMEM((total, size), jnp.float32),
            pltpu.VMEM((total, size), jnp.float32),
            pltpu.SemaphoreType.DMA((2, steps)),
            pltpu.SemaphoreType.DMA((2, steps)),
            pltpu.SemaphoreType.DMA((2,)),
        ],
        compiler_params=pltpu.CompilerParams(
            collective_id=0, has_side_effects=True, vmem_limit_bytes=48 * 1024 * 1024
        ),
        name="exchange",
    )(raw_keys.reshape(flat), raw_values.reshape(flat), turn_angle.T, key_gain.reshape(1, size))
    out = jax.ShapeDtypeStruct((total, size), raw_keys.dtype)
    keys, values = pl.pallas_call(
        place_kernel,
        out_shape=(out, out),
        in_specs=[pl.BlockSpec(memory_space=pltpu.VMEM)] * 2,
        out_specs=[pl.BlockSpec(memory_space=pl.ANY)] * 2,
        scratch_shapes=[pltpu.SemaphoreType.DMA((2,))],
        compiler_params=pltpu.CompilerParams(vmem_limit_bytes=12 * 1024 * 1024),
        name="place",
    )(keys, values)
    full = (1, positions * devices, heads, size)
    return keys.reshape(full), values.reshape(full), scale.reshape(1, heads, size)


def solution(mesh):
    in_specs = (
        P(None, (FAR, NEAR), "model", None),
        P(None, (FAR, NEAR), "model", None),
        P(),
        P(),
    )
    out_specs = (
        P((FAR, NEAR), None, "model", None),
        P((FAR, NEAR), None, "model", None),
        P((FAR, NEAR), "model", None),
    )
    body = functools.partial(local, mesh.shape[FAR], mesh.shape[NEAR])
    return jax.shard_map(body, mesh=mesh, in_specs=in_specs, out_specs=out_specs, check_vma=False)
```

time: 148 us -> 103 us (0.70)
  Pallas kernels: 0 us -> 101 us
  other arithmetic: 81 us -> 0 us
  waiting for transfers between devices: 32.3 us -> 0 us
  local copies, waits for them, and re-layouts: 23.7 us -> 0.57 us
  starting transfers between devices: 9.8 us -> 0 us
    pallas_call x0 -> x2, Pallas kernels: none -> 101 us  [the longest x1 97.9 us: local(): pl.pallas_call(functools.partial(exchange_kernel, far_size, near_size, he...]
    all_to_all x2 -> x0, waiting for transfers between devices: 32.3 us -> none  [the longest x1 32.3 us: local(): lax.all_to_all(raw_keys, ('farcp', 'nearcp'), split_axis=0, concat_axis=1...]
    sub x1 -> x0, other arithmetic: 19 us -> none  [apply_rotary(): first * cosine - second * sine]
    convert_element_type x2 -> x0, other arithmetic: 18.5 us -> none  [the longest x1 10.2 us: local(): narrow_keys = (turned_keys / key_scale[:, None]).astype(jnp.bfloat16)]
    mul x1 -> x0, other arithmetic: 17.6 us -> none  [scale_rows(): vectors * lax.rsqrt(jnp.mean(vectors * vectors, axis=-1, keepdims=True) +...]
    cos x2 -> x0, local copies, waits for them, and re-layouts: 13.2 us -> none  [apply_rotary(): jnp.cos(angle)[None, :, None, :]]
    reduce_max x1 -> x0, other arithmetic: 12.7 us -> none  [local(): key_scale = jnp.max(jnp.abs(turned_keys), axis=1)]
    reduce_sum x1 -> x0, other arithmetic: 10.6 us -> none  [scale_rows(): jnp.mean(vectors * vectors, axis=-1, keepdims=True) + 1e-06]
  transfers between devices with their start and end apart: 2 -> 0, of which waited for: 1 -> 0; matrix products, arithmetic and copies ran while one was open for 66% -> 0% of each run, Pallas kernels for 0% -> 0%
where the time goes in v1:
time: 103 us
  Pallas kernels  101 us (98%)
    pallas_call x1, Pallas kernels, local(): pl.pallas_call(functools.partial(exchange_kernel, far_size, near_size, he...  97.9 us
    pallas_call x1, Pallas kernels, local(): pl.pallas_call(place_kernel, out_shape=(out, out), in_specs=[pl.BlockSpec...  3.41 us

profile of v1, /device:TPU:0, one launch (start us, length us, event | category | flops | bytes accessed | tf_op | source)
XLA Modules:
  0.0 102.6 jit_solution(15243056414213510548)
XLA Ops:
  0.6 97.9 %exchange.1 = (bf16[16384,128]{1,0:T(8,128)(2,1)S(1)}, bf16[16384,128]{1,0:T(8,128)(2,1)S(1)}, f32[2,128]{1,0:T(2,128)}) custom-call(bf16[8,2048,128]{2,1,0:T(8,128)(2,1)} %bitcast.7, bf16[8,2048,128]{2,1,0:T(8,128)(2,1)} %bitcast.8, f32[64,8192]{1,0:T(8,128)} %bitcast.9, f32[1,128]{1,0:T(1,128)} %bitcast.11), custom_call_target="tpu_custom_call" | custom-call | tf_op jit(solution)/shard_map/exchange/pallas_call | solution.py:156
  98.6 0.0 copy-start
  98.6 3.4 %place.1 = (bf16[16384,128]{1,0:T(8,128)(2,1)}, bf16[16384,128]{1,0:T(8,128)(2,1)}) custom-call(bf16[16384,128]{1,0:T(8,128)(2,1)S(1)} %get-tuple-element.8.keys_ref, bf16[16384,128]{1,0:T(8,128)(2,1)S(1)} %get-tuple-element.9.values_ref), custom_call_target="tpu_custom_call" | custom-call | tf_op jit(solution)/shard_map/place/pallas_call | solution.py:185
  102.0 0.0 copy-done
  102.0 0.6 copy.8
Async XLA Ops:
  98.6 3.4 %copy-start = (f32[2,128]{1,0:T(2,128)S(1)}, f32[2,128]{1,0:T(2,128)}, u32[]{:S(2)}) copy-start(f32[2,128]{1,0:T(2,128)} %get-tuple-element.12) | copy-start | bytes 3076

commit v2 on v1

--- a/solution.py
+++ b/solution.py
@@ -10,6 +10,8 @@
 FAR, NEAR = "farcp", "nearcp"
 MESH_ID = pl.DeviceIdType.MESH
 TILE = 256
+PARTS = 1
+WRITES = 4
 LANES = 128
 
 
@@ -18,62 +20,76 @@
         return (index + sign * step + size) % size
     bit = 1
     while bit < size:
-        if step & bit:
-            index = index + bit - 2 * bit * ((index // bit) % 2)
+        index = index + ((step // bit) % 2) * (bit - 2 * bit * ((index // bit) % 2))
         bit *= 2
     return index
 
 
-def partner_steps(far_size, near_size):
-    steps = [(f, n) for f in range(far_size) for n in range(near_size) if (f, n) != (0, 0)]
-    return sorted(steps, key=lambda s: (-((s[0] > 0) + (s[1] > 1)), s))
+def partner_orders(far_size, near_size):
+    both, first, second, same = [], [], [], []
+    for step in range(1, far_size * near_size):
+        far, chip = step // near_size > 0, step % near_size > 1
+        (both if far and chip else first if far else second if chip else same).append(step)
+    orders = []
+    for lists in ((both, first, second), (first, both, second)):
+        order = []
+        for turn in range(max(map(len, lists))):
+            order += [steps[turn] for steps in lists if turn < len(steps)]
+        orders.append(order + same)
+    return orders
 
 
 def exchange_kernel(
-    far_size, near_size, heads, keys_ref, values_ref, angle_ref, gain_ref,
+    far_size, near_size, heads, keys_ref, values_ref, turn_ref, gain_ref,
     out_keys, out_values, out_scale,
-    landed, cos_table, sin_table, turned, send_sem, recv_sem, local_sem,
+    angle_ref, landed, cos_table, sin_table, turned, send_sem, recv_sem, local_sem,
 ):
     far, near = lax.axis_index(FAR), lax.axis_index(NEAR)
     me = far * near_size + near
     rows = keys_ref.shape[1]
     total_rows = landed.shape[0]
     half = angle_ref.shape[0]
-    steps = partner_steps(far_size, near_size)
+    even, odd = partner_orders(far_size, near_size)
+    part = rows // PARTS
 
     def device(step, sign):
         return (
-            moved_index(far, step[0], far_size, sign),
-            moved_index(near, step[1], near_size, sign),
+            moved_index(far, step // near_size, far_size, sign),
+            moved_index(near, step % near_size, near_size, sign),
         )
 
     barrier = pltpu.get_barrier_semaphore()
-    for step in steps:
+    for step in even:
         f, n = device(step, 1)
         pl.semaphore_signal(barrier, inc=1, device_id={FAR: f, NEAR: n}, device_id_type=MESH_ID)
+    angles = pltpu.make_async_copy(turn_ref, angle_ref, local_sem.at[2])
+    angles.start()
     own = [
         pltpu.make_async_copy(src.at[me], dst.at[pl.ds(me * rows, rows)], local_sem.at[i])
         for i, (src, dst) in enumerate(((keys_ref, landed), (values_ref, out_values)))
     ]
     for copy in own:
         copy.start()
-    pl.semaphore_wait(barrier, len(steps))
-
-    copies = [[], []]
-    for which, (src, dst) in enumerate(((keys_ref, landed), (values_ref, out_values))):
-        for i, step in enumerate(steps):
-            f, n = device(step, 1)
-            copy = pltpu.make_async_remote_copy(
-                src_ref=src.at[f * near_size + n],
-                dst_ref=dst.at[pl.ds(me * rows, rows)],
-                send_sem=send_sem.at[which, i],
-                recv_sem=recv_sem.at[which, i],
-                device_id={FAR: f, NEAR: n},
-                device_id_type=MESH_ID,
-            )
-            copy.start()
-            copies[which].append(copy)
-
+
+    def remote(which, piece, step):
+        src, dst = ((keys_ref, landed), (values_ref, out_values))[which]
+        f, n = device(step, 1)
+        return pltpu.make_async_remote_copy(
+            src_ref=src.at[f * near_size + n, pl.ds(piece * part, part)],
+            dst_ref=dst.at[pl.ds(me * rows + piece * part, part)],
+            send_sem=send_sem.at[which, piece, step],
+            recv_sem=recv_sem.at[which, piece, step],
+            device_id={FAR: f, NEAR: n},
+            device_id_type=MESH_ID,
+        )
+
+    pl.semaphore_wait(barrier, len(even))
+    for which in range(2):
+        for piece in range(PARTS):
+            for a, b in zip(even, odd):
+                remote(which, piece, a + (b - a) * (me % 2)).start()
+
+    angles.wait()
     gain = gain_ref[...]
     other_gain = pltpu.roll(gain, half, 1)
 
@@ -105,9 +121,10 @@
     largest = jnp.zeros((8, LANES), jnp.float32)
     own[0].wait()
     largest = prepare(me, largest)
-    for i in reversed(range(len(steps))):
-        copies[0][i].wait_recv()
-        f, n = device(steps[i], -1)
+    for step in even[::-1]:
+        for piece in range(PARTS):
+            remote(0, piece, step).wait_recv()
+        f, n = device(step, -1)
         largest = prepare(f * near_size + n, largest)
 
     head_of = lax.broadcasted_iota(jnp.int32, (8, LANES), 0) % heads
@@ -127,18 +144,22 @@
     lax.fori_loop(0, total_rows // TILE, narrow, 0)
 
     own[1].wait()
-    for copy in copies[1]:
-        copy.wait_recv()
-    for group in copies:
-        for copy in group:
-            copy.wait_send()
-
-
-def place_kernel(keys_ref, values_ref, out_keys, out_values, sem):
-    copies = [
-        pltpu.make_async_copy(keys_ref, out_keys, sem.at[0]),
-        pltpu.make_async_copy(values_ref, out_values, sem.at[1]),
-    ]
+    for piece in range(PARTS):
+        for step in even:
+            remote(1, piece, step).wait_recv()
+    for which in range(2):
+        for piece in range(PARTS):
+            for step in even:
+                remote(which, piece, step).wait_send()
+
+
+def place_kernel(keys_ref, values_ref, scale_ref, out_keys, out_values, out_scale, sem):
+    part = keys_ref.shape[0] // WRITES
+    copies = [pltpu.make_async_copy(scale_ref, out_scale, sem.at[2, 0])]
+    for i, (src, dst) in enumerate(((keys_ref, out_keys), (values_ref, out_values))):
+        for j in range(WRITES):
+            place = pl.ds(j * part, part)
+            copies.append(pltpu.make_async_copy(src.at[place], dst.at[place], sem.at[i, j]))
     for copy in copies:
         copy.start()
     for copy in copies:
@@ -150,16 +171,15 @@
     devices = far_size * near_size
     rows = positions * heads
     total = rows * devices
-    steps = devices - 1
     flat = (sequences, rows, size)
     whole = pltpu.VMEM((total, size), raw_keys.dtype)
     keys, values, scale = pl.pallas_call(
         functools.partial(exchange_kernel, far_size, near_size, heads),
-        out_shape=(whole, whole, jax.ShapeDtypeStruct((heads, size), jnp.float32)),
+        out_shape=(whole, whole, pltpu.VMEM((heads, size), jnp.float32)),
         in_specs=[
             pl.BlockSpec(memory_space=pl.ANY),
             pl.BlockSpec(memory_space=pl.ANY),
-            pl.BlockSpec(memory_space=pltpu.VMEM),
+            pl.BlockSpec(memory_space=pl.ANY),
             pl.BlockSpec(memory_space=pltpu.VMEM),
         ],
         out_specs=(
@@ -168,13 +188,14 @@
             pl.BlockSpec(memory_space=pltpu.VMEM),
         ),
         scratch_shapes=[
+            pltpu.VMEM((size // 2, total // heads), jnp.float32),
             pltpu.VMEM((total, size), raw_keys.dtype),
             pltpu.VMEM((total, size), jnp.float32),
             pltpu.VMEM((total, size), jnp.float32),
             pltpu.VMEM((total, size), jnp.float32),
-            pltpu.SemaphoreType.DMA((2, steps)),
-            pltpu.SemaphoreType.DMA((2, steps)),
-            pltpu.SemaphoreType.DMA((2,)),
+            pltpu.SemaphoreType.DMA((2, PARTS, devices)),
+            pltpu.SemaphoreType.DMA((2, PARTS, devices)),
+            pltpu.SemaphoreType.DMA((3,)),
         ],
         compiler_params=pltpu.CompilerParams(
             collective_id=0, has_side_effects=True, vmem_limit_bytes=48 * 1024 * 1024
@@ -182,15 +203,15 @@
         name="exchange",
     )(raw_keys.reshape(flat), raw_values.reshape(flat), turn_angle.T, key_gain.reshape(1, size))
     out = jax.ShapeDtypeStruct((total, size), raw_keys.dtype)
-    keys, values = pl.pallas_call(
+    keys, values, scale = pl.pallas_call(
         place_kernel,
-        out_shape=(out, out),
-        in_specs=[pl.BlockSpec(memory_space=pltpu.VMEM)] * 2,
-        out_specs=[pl.BlockSpec(memory_space=pl.ANY)] * 2,
-        scratch_shapes=[pltpu.SemaphoreType.DMA((2,))],
+        out_shape=(out, out, jax.ShapeDtypeStruct((heads, size), jnp.float32)),
+        in_specs=[pl.BlockSpec(memory_space=pltpu.VMEM)] * 3,
+        out_specs=[pl.BlockSpec(memory_space=pl.ANY)] * 3,
+        scratch_shapes=[pltpu.SemaphoreType.DMA((3, WRITES))],
         compiler_params=pltpu.CompilerParams(vmem_limit_bytes=12 * 1024 * 1024),
         name="place",
-    )(keys, values)
+    )(keys, values, scale)
     full = (1, positions * devices, heads, size)
     return keys.reshape(full), values.reshape(full), scale.reshape(1, heads, size)
 

time: 103 us -> 100 us (0.971)
  Pallas kernels: 101 us -> 99.5 us
    pallas_call x1, Pallas kernels: 97.9 us -> 96.1 us  [local(): pl.pallas_call(functools.partial(exchange_kernel, far_size, near_size, he...]
where the time goes in v2:
time: 100 us
  Pallas kernels  99.5 us (100%)
    pallas_call x1, Pallas kernels, local(): pl.pallas_call(functools.partial(exchange_kernel, far_size, near_size, he...  96.1 us
    pallas_call x1, Pallas kernels, local(): pl.pallas_call(place_kernel, out_shape=(out, out, jax.ShapeDtypeStruct((h...  3.41 us

profile of v2, /device:TPU:0, one launch (start us, length us, event | category | flops | bytes accessed | tf_op | source)
XLA Modules:
  0.0 100.2 jit_solution(16355774280191218173)
XLA Ops:
  0.6 96.1 %exchange.1 = (bf16[16384,128]{1,0:T(8,128)(2,1)S(1)}, bf16[16384,128]{1,0:T(8,128)(2,1)S(1)}, f32[2,128]{1,0:T(2,128)S(1)}) custom-call(bf16[8,2048,128]{2,1,0:T(8,128)(2,1)} %bitcast.7, bf16[8,2048,128]{2,1,0:T(8,128)(2,1)} %bitcast.8, f32[64,8192]{1,0:T(8,128)} %bitcast.9, f32[1,128]{1,0:T(1,128)} %bitcast.10), custom_call_target="tpu_custom_call" | custom-call | tf_op jit(solution)/shard_map/exchange/pallas_call | solution.py:176
  96.8 3.4 %place.1 = (bf16[16384,128]{1,0:T(8,128)(2,1)}, bf16[16384,128]{1,0:T(8,128)(2,1)}, f32[2,128]{1,0:T(2,128)}) custom-call(bf16[16384,128]{1,0:T(8,128)(2,1)S(1)} %get-tuple-element.9.keys_ref, bf16[16384,128]{1,0:T(8,128)(2,1)S(1)} %get-tuple-element.10.values_ref, f32[2,128]{1,0:T(2,128)S(1)} %get-tuple-element.11.scale_ref), custom_call_target="tpu_custom_call" | custom-call | tf_op jit(solution)/shard_map/place/pallas_call | solution.py:206
